TPU v7x, 32 devices: a whole 2x2x4 slice. The times are simulated.
32 devices in a mesh: batch: 4 (over y, core), tensor: 2 (over x), latent: 4 (over z).
Axes of the slice: x: 2, y: 2, z: 4, core: 2. Of those that a mesh axis runs over, the one named last changes fastest.
Arguments:
- residual: bfloat16 [1024, 3584], P('batch', ('tensor', 'latent')), may hold values from -6 to 6
- target: bfloat16 [1024, 3584], P('batch', ('tensor', 'latent')), may hold values from -6 to 6
- encoder_weight: bfloat16 [3584, 32768], P(None, ('tensor', 'latent')), may hold values from -0.09375 to 0.09375
- encoder_bias: bfloat16 [32768], P(('tensor', 'latent')), may hold values from -0.59765625 to 0.29882812
- decoder_weight: bfloat16 [32768, 3584], P(('tensor', 'latent')), may hold values from -0.0625 to 0.0625
- decoder_bias: bfloat16 [3584], replicated, may hold values from -3 to 3
- first_gain: bfloat16 [3584], replicated, may hold values from 0.5 to 1.5
- second_gain: bfloat16 [3584], replicated, may hold values from 0.5 to 1.5
- gate_weight: bfloat16 [3584, 7168], P(None, ('tensor', 'latent')), may hold values from -0.09375 to 0.09375
- up_weight: bfloat16 [3584, 7168], P(None, ('tensor', 'latent')), may hold values from -0.09375 to 0.09375
- down_weight: bfloat16 [7168, 3584], P(('tensor', 'latent')), may hold values from -0.09375 to 0.09375
Outputs:
- encoder_grad: bfloat16 [3584, 32768], P('batch', ('tensor', 'latent'))
- decoder_grad: bfloat16 [32768, 3584], P(('tensor', 'latent'), 'batch')
All inputs are finite; a program needn't handle non-finite values.
Results may differ from a plain program's by a relative error of at most 0.012.
The roundings to bfloat16 on the way count: a program that leaves them out, or rounds other values in their place, can miss the bound.
Values may be sent and summed in bfloat16 or wider, within the bound.
A program may use at most 192 MiB of HBM per device.

v0:
```python
import jax
import jax.numpy as jnp
from jax import lax
from jax.sharding import PartitionSpec as P

epsilon = 1e-06


def per_device(
    residual,
    target,
    encoder_weight,
    encoder_bias,
    decoder_weight,
    decoder_bias,
    first_gain,
    second_gain,
    gate_weight,
    up_weight,
    down_weight,
):
    f32 = jnp.float32
    bf16 = jnp.bfloat16
    contract_last = (((1,), (1,)), ((), ()))
    contract_first = (((0,), (0,)), ((), ()))
    share_width = residual.shape[1]
    model_width = share_width * lax.axis_size(("tensor", "latent"))
    offset = lax.axis_index(("tensor", "latent")) * share_width
    token_count = residual.shape[0] * lax.axis_size("batch")
    bias_share = lax.dynamic_slice_in_dim(decoder_bias.astype(f32), offset, share_width)
    first_share = lax.dynamic_slice_in_dim(first_gain.astype(f32), offset, share_width)
    second_share = lax.dynamic_slice_in_dim(second_gain.astype(f32), offset, share_width)
    centered_share = (residual.astype(f32) - bias_share).astype(bf16)
    centered = lax.all_gather(centered_share, ("tensor", "latent"), axis=1, tiled=True)
    preact = jnp.dot(centered, encoder_weight, preferred_element_type=f32) + encoder_bias.astype(
        f32
    )
    latents = jnp.maximum(preact, 0.0).astype(bf16)
    partial_recon = jnp.dot(latents, decoder_weight, preferred_element_type=f32)
    recon_full = lax.psum(partial_recon.astype(jnp.bfloat16), ("tensor", "latent")).astype(
        jnp.float32
    ) + decoder_bias.astype(f32)
    scale_in = lax.rsqrt(
        jnp.sum(recon_full * recon_full, axis=1, keepdims=True) / model_width + epsilon
    )
    normed_input = (recon_full * scale_in * first_gain.astype(f32)).astype(bf16)
    recon = lax.dynamic_slice_in_dim(recon_full, offset, share_width, 1)
    gate_value = jnp.dot(normed_input, gate_weight, preferred_element_type=f32)
    up_value = jnp.dot(normed_input, up_weight, preferred_element_type=f32)
    gelu_value, gelu_back = jax.vjp(lambda v: jax.nn.gelu(v, approximate=True), gate_value)
    hidden = (gelu_value * up_value).astype(bf16)
    partial_out = jnp.dot(hidden, down_weight, preferred_element_type=f32)
    output = lax.psum_scatter(
        partial_out.astype(jnp.bfloat16), ("tensor", "latent"), scatter_dimension=1, tiled=True
    ).astype(jnp.float32)
    out_squares = lax.psum(jnp.sum(output * output, axis=1), ("tensor", "latent"))
    scale_out = lax.rsqrt(out_squares[:, None] / model_width + epsilon)
    normed_out = output * scale_out
    result = recon + normed_out * second_share
    grad_result = 2.0 * (result - target.astype(f32)) / token_count
    grad_normed = grad_result * second_share
    inner_out = (
        lax.psum(jnp.sum(grad_normed * normed_out, axis=1), ("tensor", "latent")) / model_width
    )
    grad_share = (scale_out * (grad_normed - normed_out * inner_out[:, None])).astype(bf16)
    grad_output = lax.all_gather(grad_share, ("tensor", "latent"), axis=1, tiled=True)
    grad_hidden = lax.dot_general(
        grad_output, down_weight, contract_last, preferred_element_type=f32
    )
    grad_gate = gelu_back(grad_hidden * up_value)[0].astype(bf16)
    grad_up = (grad_hidden * gelu_value).astype(bf16)
    partial_input = lax.dot_general(
        grad_gate, gate_weight, contract_last, preferred_element_type=f32
    )
    partial_input = partial_input + lax.dot_general(
        grad_up, up_weight, contract_last, preferred_element_type=f32
    )
    grad_normed_in = lax.psum_scatter(
        partial_input.astype(jnp.bfloat16), ("tensor", "latent"), scatter_dimension=1, tiled=True
    ).astype(jnp.float32)
    unit = recon * scale_in
    grad_unit = grad_normed_in * first_share
    inner_in = lax.psum(jnp.sum(grad_unit * unit, axis=1), ("tensor", "latent")) / model_width
    recon_share = (grad_result + scale_in * (grad_unit - unit * inner_in[:, None])).astype(bf16)
    grad_recon = lax.all_gather(recon_share, ("tensor", "latent"), axis=1, tiled=True)
    grad_latent = lax.dot_general(
        grad_recon, decoder_weight, contract_last, preferred_element_type=f32
    )
    grad_preact = jnp.where(preact > 0, grad_latent, 0.0).astype(bf16)
    centered_block, recon_block = (
        lax.all_to_all(centered, "batch", split_axis=1, concat_axis=0, tiled=True),
        lax.all_to_all(grad_recon, "batch", split_axis=1, concat_axis=0, tiled=True),
    )
    latents_all, preact_all = (
        lax.all_gather(latents, "batch", axis=0, tiled=True),
        lax.all_gather(grad_preact, "batch", axis=0, tiled=True),
    )
    encoder_grad = lax.dot_general(
        centered_block, preact_all, contract_first, preferred_element_type=f32
    )
    decoder_grad = lax.dot_general(
        latents_all, recon_block, contract_first, preferred_element_type=f32
    )
    return (encoder_grad.astype(bf16), decoder_grad.astype(bf16))


def solution(mesh):
    in_specs = (
        P("batch", ("tensor", "latent")),
        P("batch", ("tensor", "latent")),
        P(None, ("tensor", "latent")),
        P(("tensor", "latent")),
        P(("tensor", "latent"), None),
        P(),
        P(),
        P(),
        P(None, ("tensor", "latent")),
        P(None, ("tensor", "latent")),
        P(("tensor", "latent"), None),
    )
    out_specs = (P("batch", ("tensor", "latent")), P(("tensor", "latent"), "batch"))
    return jax.shard_map(
        per_device, mesh=mesh, in_specs=in_specs, out_specs=out_specs, check_vma=False
    )
```

profile of v0, /device:TPU:0, one launch (start us, length us, event | category | flops | bytes accessed | tf_op | source)
XLA Modules:
  0.0 670.3 jit_solution(1007464066563289429)
XLA Ops:
  10.5 49.3 %all-gather.6.cloned.1.call-done = bf16[256,3584]{0,1:T(8,128)(2,1)} async-done(((bf16[256,448]{0,1:T(8,128)(2,1)}), bf16[256,3584]{0,1:T(8,128)(2,1)}) %all-gather.6.cloned.1.call-update) | async-done | bytes 1835024 | tf_op jit(solution)/shard_map/all_gather | solution.py:34
  59.8 15.2 %maximum_convert_fusion = (bf16[256,4096]{1,0:T(8,128)(2,1)S(1)}, f32[256,4096]{1,0:T(8,128)}) fusion(f32[4096]{0:T(1024)S(1)} %convert_element_type.74, bf16[256,3584]{0,1:T(8,128)(2,1)} %all-gather.6.cloned.1.call-done, bf16[3584,4096]{1,0:T(8,128)(2,1)} %param.13), kind=kOutput, calls=%fused_computation.11 | convolution fusion | flops 7519338496 | bytes 37502976 | tf_op jit(solution)/shard_map/dot_general | solution.py:35
  75.0 15.5 %convolution_convert_fusion.2 = bf16[256,3584]{1,0:T(8,128)(2,1)} fusion(bf16[256,4096]{1,0:T(8,128)(2,1)S(1)} %get-tuple-element.4, bf16[4096,3584]{1,0:T(8,128)(2,1)} %param.15), kind=kOutput, calls=%fused_computation.5 | convolution fusion | flops 7517110272 | bytes 33292288 | tf_op jit(solution)/shard_map/dot_general | solution.py:39
  90.7 94.5 %all-reduce.2.cloned.1.call-done = bf16[256,3584]{1,0:T(8,128)(2,1)} async-done(((bf16[256,3584]{1,0:T(8,128)(2,1)}), bf16[256,3584]{1,0:T(8,128)(2,1)}) %all-reduce.2.cloned.1.call-update) | async-done | bytes 1835024 | tf_op jit(solution)/shard_map/psum | solution.py:40
  185.2 4.0 convert_add_fusion
  189.2 5.6 fusion.30
  197.1 4.3 fusion.2
  203.1 64.5 %reduce-scatter.7.cloned.1.call-done = bf16[448,256]{1,0:T(8,128)(2,1)} async-done(((bf16[3584,256]{1,0:T(8,128)(2,1)}), bf16[448,256]{1,0:T(8,128)(2,1)}) %reduce-scatter.7.cloned.1.call-update) | async-done | bytes 229392
  268.9 19.4 %psum.29 = f32[256]{0:T(256)S(1)} all-reduce(f32[256]{0:T(256)S(1)} %fusion.20), channel_id=1, replica_groups=mesh['batch'=4,'tensor'=2,'latent'=4] {'tensor','latent'}, use_global_device_ids=true, to_apply=%region_4.0 | all-reduce | flops 256 | bytes 2048 | tf_op jit(solution)/shard_map/psum | solution.py:56
  289.7 17.2 %psum.30 = f32[256]{0:T(256)S(1)} all-reduce(f32[256]{0:T(256)S(1)} %fusion.16), channel_id=1, replica_groups=mesh['batch'=4,'tensor'=2,'latent'=4] {'tensor','latent'}, use_global_device_ids=true, to_apply=%region_6.0 | all-reduce | flops 256 | bytes 2048 | tf_op jit(solution)/shard_map/psum | solution.py:63
  309.5 45.8 %all-gather.8.cloned.1.call-done = bf16[256,3584]{0,1:T(8,128)(2,1)} async-done(((bf16[256,448]{0,1:T(8,128)(2,1)}), bf16[256,3584]{0,1:T(8,128)(2,1)}) %all-gather.8.cloned.1.call-update) | async-done | bytes 1835024 | tf_op jit(solution)/shard_map/all_gather | solution.py:66
  355.3 5.6 fusion.45
  361.0 5.4 fusion.21
  366.5 3.6 fusion.3
  370.3 65.2 %reduce-scatter.9.cloned.1.call-done = bf16[448,256]{1,0:T(8,128)(2,1)} async-done(((bf16[3584,256]{1,0:T(8,128)(2,1)}), bf16[448,256]{1,0:T(8,128)(2,1)}) %reduce-scatter.9.cloned.1.call-update) | async-done | bytes 229392
  438.0 19.3 %psum.31 = f32[256]{0:T(256)S(1)} all-reduce(f32[256]{0:T(256)S(1)} %multiply_reduce_fusion.1), channel_id=1, replica_groups=mesh['batch'=4,'tensor'=2,'latent'=4] {'tensor','latent'}, use_global_device_ids=true, to_apply=%region_9.0 | all-reduce | flops 256 | bytes 2048 | tf_op jit(solution)/shard_map/psum | solution.py:83
  460.5 44.0 %all-gather.10.cloned.1.call-done = bf16[256,3584]{0,1:T(8,128)(2,1)} async-done(((bf16[256,448]{0,1:T(8,128)(2,1)}), bf16[256,3584]{0,1:T(8,128)(2,1)}) %all-gather.10.cloned.1.call-update) | async-done | bytes 1835024 | tf_op jit(solution)/shard_map/all_gather | solution.py:85
  504.5 18.3 %fusion = bf16[256,4096]{1,0:T(8,128)(2,1)} fusion(bf16[256,3584]{0,1:T(8,128)(2,1)} %all-gather.10.cloned.1.call-done, bf16[4096,3584]{1,0:T(8,128)(2,1)} %param.15, f32[256,4096]{1,0:T(8,128)} %get-tuple-element.5), kind=kOutput, calls=%fused_computation.6 | convolution fusion | flops 7519338496 | bytes 37486592 | tf_op jit(solution)/shard_map/dot_general | solution.py:86
  522.8 46.2 %all_to_all.38 = bf16[256,4,896]{0,2,1:T(8,128)(2,1)} all-to-all(bf16[256,4,896]{0,2,1:T(8,128)(2,1)S(1)} %bitcast.35), channel_id=1, replica_groups=mesh['batch'=4,'tensor'=2,'latent'=4] {'batch'}, dimensions={1} | all-to-all | bytes 3670016 | tf_op jit(solution)/shard_map/all_to_all | solution.py:91
  569.0 3.8 all-to-all-start.1
  576.5 24.1 %all-to-all-done.1 = bf16[256,4,896]{0,2,1:T(8,128)(2,1)S(1)} async-done(((bf16[256,4,896]{0,2,1:T(8,128)(2,1)}), bf16[256,4,896]{0,2,1:T(8,128)(2,1)S(1)}, u32[]{:S(2)}, u32[]{:S(2)}) %all-to-all-start.1) | async-done | bytes 1835040 | tf_op jit(solution)/shard_map/all_to_all | solution.py:92
  603.0 15.2 %convolution_convert_fusion = bf16[4096,896]{1,0:T(8,128)(2,1)} fusion(bf16[1024,4096]{1,0:T(8,128)(2,1)} %all-gather.14.cloned.1.call-done, bf16[1024,896]{1,0:T(8,128)(2,1)} %bitcast.38), kind=kOutput, calls=%fused_computation | convolution fusion | flops 7519862784 | bytes 17563648 | tf_op jit(solution)/shard_map/dot_general | solution.py:101
  618.1 33.3 %all-gather.12.cloned.1.call-done = bf16[1024,4096]{1,0:T(8,128)(2,1)} async-done(((bf16[256,4096]{1,0:T(8,128)(2,1)}), bf16[1024,4096]{1,0:T(8,128)(2,1)}) %all-gather.12.cloned.1.call-update) | async-done | bytes 8388624 | tf_op jit(solution)/shard_map/all_gather | solution.py:96
  651.4 12.1 %convolution_convert_fusion.1 = bf16[896,4096]{1,0:T(8,128)(2,1)} fusion(bf16[1024,896]{1,0:T(8,128)(2,1)S(1)} %bitcast.37, bf16[1024,4096]{1,0:T(8,128)(2,1)} %all-gather.12.cloned.1.call-done), kind=kOutput, calls=%fused_computation.1 | convolution fusion | flops 7519862784 | bytes 17563648 | tf_op jit(solution)/shard_map/dot_general | solution.py:98
  (71 shorter events, 24.4 us)
Async XLA Ops:
  7.2 52.6 %all-gather.6.cloned.1.call-start = ((), (), s32[]{:S(2)}) async-start(), calls=%async_computation.4 | async-start | bytes 2064384 | tf_op jit(solution)/shard_map/all_gather | solution.py:34
  9.8 175.5 %all-reduce.2.cloned.1.call-start = ((), (), s32[]{:S(2)}) async-start(), calls=%async_computation.5 | async-start | bytes 3670016 | tf_op jit(solution)/shard_map/psum | solution.py:40
  75.0 15.5 %copy-start = (bf16[256,4096]{1,0:T(8,128)(2,1)}, bf16[256,4096]{1,0:T(8,128)(2,1)S(1)}, u32[]{:S(2)}) copy-start(bf16[256,4096]{1,0:T(8,128)(2,1)S(1)} %get-tuple-element.4) | copy-start | bytes 6291460
  75.0 15.8 %copy-start.5 = (bf16[3584]{0:T(1024)(128)(2,1)S(1)}, bf16[3584]{0:T(1024)(128)(2,1)}, u32[]{:S(2)}) copy-start(bf16[3584]{0:T(1024)(128)(2,1)} %param.16) | copy-start | bytes 21508
  75.0 15.8 %copy-start.6 = (bf16[3584]{0:T(1024)(128)(2,1)S(1)}, bf16[3584]{0:T(1024)(128)(2,1)}, u32[]{:S(2)}) copy-start(bf16[3584]{0:T(1024)(128)(2,1)} %param.17) | copy-start | bytes 21508
  90.5 177.2 %reduce-scatter.7.cloned.1.call-start = ((), (), s32[]{:S(2)}) async-start(), calls=%async_computation.10 | async-start | bytes 2064384
  185.2 9.6 %slice-start = ((s8[6422528]{0:T(1024)(128)(4,1)}), s8[4194304]{0:T(1024)(128)(4,1)S(1)}, s32[]{:S(2)}) async-start(s8[6422528]{0:T(1024)(128)(4,1)} %bitcast.29), calls=%async_computation.12 | async-start | bytes 8388608
  189.2 5.7 slice-start.1
  189.2 5.7 copy-start.3
  189.2 7.9 %slice-start.4 = ((s8[6422528]{0:T(1024)(128)(4,1)}), s8[4194304]{0:T(1024)(128)(4,1)S(1)}, s32[]{:S(2)}) async-start(s8[6422528]{0:T(1024)(128)(4,1)} %bitcast.41), calls=%async_computation.16 | async-start | bytes 8388608
  194.9 2.2 slice-start.5
  197.1 4.4 copy-start.4
  201.4 154.0 %all-gather.8.cloned.1.call-start = ((), (), s32[]{:S(2)}) async-start(), calls=%async_computation.6 | async-start | bytes 2064384 | tf_op jit(solution)/shard_map/all_gather | solution.py:66
  309.2 126.3 %reduce-scatter.9.cloned.1.call-start = ((), (), s32[]{:S(2)}) async-start(), calls=%async_computation.11 | async-start | bytes 2064384
  355.3 11.1 %slice-start.2 = ((s8[6422528]{0:T(1024)(128)(4,1)}), s8[2228224]{0:T(1024)(128)(4,1)S(1)}, s32[]{:S(2)}) async-start(s8[6422528]{0:T(1024)(128)(4,1)} %bitcast.31), calls=%async_computation.14 | async-start | bytes 4456448
  361.0 5.5 slice-start.3
  370.1 134.3 %all-gather.10.cloned.1.call-start = ((), (), s32[]{:S(2)}) async-start(), calls=%async_computation.7 | async-start | bytes 2064384 | tf_op jit(solution)/shard_map/all_gather | solution.py:85
  459.7 143.3 %all-gather.14.cloned.1.call-start = ((), (), s32[]{:S(2)}) async-start(), calls=%async_computation.9 | async-start | bytes 10485760 | tf_op jit(solution)/shard_map/all_gather | solution.py:95
  460.4 191.0 %all-gather.12.cloned.1.call-start = ((), (), s32[]{:S(2)}) async-start(), calls=%async_computation.8 | async-start | bytes 10485760 | tf_op jit(solution)/shard_map/all_gather | solution.py:96
  504.5 18.4 %copy-start.1 = (bf16[256,3584]{0,1:T(8,128)(2,1)S(1)}, bf16[256,3584]{0,1:T(8,128)(2,1)}, u32[]{:S(2)}) copy-start(bf16[256,3584]{0,1:T(8,128)(2,1)} %all-gather.6.cloned.1.call-done) | copy-start | bytes 5505028
  569.0 31.6 %all-to-all-start.1 = ((bf16[256,4,896]{0,2,1:T(8,128)(2,1)}), bf16[256,4,896]{0,2,1:T(8,128)(2,1)S(1)}, u32[]{:S(2)}, u32[]{:S(2)}) async-start(bf16[256,4,896]{0,2,1:T(8,128)(2,1)} %bitcast.36), calls=%async_computation.1 | async-start | bytes 3670016 | tf_op jit(solution)/shard_map/all_to_all | solution.py:92
  603.0 48.5 %copy-start.2 = (bf16[4,256,896]{2,1,0:T(8,128)(2,1)S(1)}, bf16[4,256,896]{2,1,0:T(8,128)(2,1)}, u32[]{:S(2)}) copy-start(bf16[4,256,896]{2,1,0:T(8,128)(2,1)} %copy.34) | copy-start | bytes 5505028
Sparse Core Ops, SparseCore 0:
  10.6 49.1 all-gather.5
  90.6 94.5 all-reduce.1
  201.5 66.1 reduce-scatter.6
  309.4 45.9 all-gather.7
  370.3 65.1 reduce-scatter.8
  459.8 44.6 all-gather.9
  506.0 81.8 all-gather.13
  590.1 61.2 all-gather.11
where the time goes:
time: 671 us; the launch traced here: 670 us
  waiting for transfers between devices  422 us (63%)
  matrix products  103 us (15%)
  blocking collectives  102 us (15%)
  between operations  14.4 us (2%)
  other arithmetic  13.9 us (2%)
  local copies, waits for them, and re-layouts  10.9 us (2%)
    unnamed x10, waiting for transfers between devices  131 us
    psum x1, waiting for transfers between devices, per_device(): lax.psum(partial_recon.astype(jnp.bfloat16), ('tensor', 'latent'))  94.5 us
    all_gather x1, waiting for transfers between devices, per_device(): lax.all_gather(centered_share, ('tensor', 'latent'), axis=1, tiled=True)  49.3 us
    all_to_all x1, blocking collectives, per_device(): lax.all_to_all(centered, 'batch', split_axis=1, concat_axis=0, tiled=True)  46.2 us
    all_gather x1, waiting for transfers between devices, per_device(): lax.all_gather(grad_share, ('tensor', 'latent'), axis=1, tiled=True)  45.8 us
    all_gather x1, waiting for transfers between devices, per_device(): lax.all_gather(recon_share, ('tensor', 'latent'), axis=1, tiled=True)  44 us
    all_gather x1, waiting for transfers between devices, per_device(): lax.all_gather(grad_preact, 'batch', axis=0, tiled=True)  33.3 us
    all_to_all x1, waiting for transfers between devices, per_device(): lax.all_to_all(grad_recon, 'batch', split_axis=1, concat_axis=0, tiled=True)  24.1 us
  transfers between devices with their start and end apart: 9, of which 8 were waited for; matrix products, arithmetic and copies ran while one was open for 6% of the time, Pallas kernels for 0%

commit v1 on v0

--- a/solution.py
+++ b/solution.py
@@ -4,6 +4,11 @@
 from jax.sharding import PartitionSpec as P
 
 epsilon = 1e-06
+
+
+def axis_by_axis(x, inner_axis, outer_axis):
+    half = lax.psum(x, inner_axis)
+    return lax.psum(half, outer_axis)
 
 
 def per_device(
@@ -37,7 +42,7 @@
     )
     latents = jnp.maximum(preact, 0.0).astype(bf16)
     partial_recon = jnp.dot(latents, decoder_weight, preferred_element_type=f32)
-    recon_full = lax.psum(partial_recon.astype(jnp.bfloat16), ("tensor", "latent")).astype(
+    recon_full = axis_by_axis(partial_recon.astype(jnp.bfloat16), "tensor", "latent").astype(
         jnp.float32
     ) + decoder_bias.astype(f32)
     scale_in = lax.rsqrt(

time: 671 us -> 712 us (1.061)
  waiting for transfers between devices: 422 us -> 463 us
    psum x1 -> x2, waiting for transfers between devices: 94.5 us -> 136 us  [the longest x1 79.7 us: axis_by_axis(): return lax.psum(half, outer_axis)]
    unnamed x10 -> x11, waiting for transfers between devices: 131 us -> 130 us
  transfers between devices with their start and end apart: 9 -> 10, of which waited for: 8 -> 9; matrix products, arithmetic and copies ran while one was open for 6% -> 6% of each run, Pallas kernels for 0% -> 0%
where the time goes in v1:
time: 712 us; the launch traced here: 711 us
  waiting for transfers between devices  463 us (65%)
  matrix products  103 us (14%)
  blocking collectives  102 us (14%)
  between operations  14.1 us (2%)
  other arithmetic  13.9 us (2%)
  local copies, waits for them, and re-layouts  10.9 us (2%)
    unnamed x11, waiting for transfers between devices  130 us
    psum x1, waiting for transfers between devices, axis_by_axis(): return lax.psum(half, outer_axis)  79.7 us
    psum x1, waiting for transfers between devices, axis_by_axis(): half = lax.psum(x, inner_axis)  56.1 us
    all_gather x1, waiting for transfers between devices, per_device(): lax.all_gather(centered_share, ('tensor', 'latent'), axis=1, tiled=True)  49.3 us
    all_to_all x1, blocking collectives, per_device(): lax.all_to_all(centered, 'batch', split_axis=1, concat_axis=0, tiled=True)  46.2 us
    all_gather x1, waiting for transfers between devices, per_device(): lax.all_gather(grad_share, ('tensor', 'latent'), axis=1, tiled=True)  45.8 us
    all_gather x1, waiting for transfers between devices, per_device(): lax.all_gather(recon_share, ('tensor', 'latent'), axis=1, tiled=True)  43.9 us
    all_gather x1, waiting for transfers between devices, per_device(): lax.all_gather(grad_preact, 'batch', axis=0, tiled=True)  33.3 us
  transfers between devices with their start and end apart: 10, of which 9 were waited for; matrix products, arithmetic and copies ran while one was open for 6% of the time, Pallas kernels for 0%

profile of v1, /device:TPU:0, one launch (start us, length us, event | category | flops | bytes accessed | tf_op | source)
XLA Modules:
  0.0 711.0 jit_solution(17441820619323511569)
XLA Ops:
  10.5 49.3 %all-gather.6.cloned.1.call-done = bf16[256,3584]{0,1:T(8,128)(2,1)} async-done(((bf16[256,448]{0,1:T(8,128)(2,1)}), bf16[256,3584]{0,1:T(8,128)(2,1)}) %all-gather.6.cloned.1.call-update) | async-done | bytes 1835024 | tf_op jit(solution)/shard_map/all_gather | solution.py:39
  59.8 15.2 %maximum_convert_fusion = (bf16[256,4096]{1,0:T(8,128)(2,1)S(1)}, f32[256,4096]{1,0:T(8,128)}) fusion(f32[4096]{0:T(1024)S(1)} %convert_element_type.74, bf16[256,3584]{0,1:T(8,128)(2,1)} %all-gather.6.cloned.1.call-done, bf16[3584,4096]{1,0:T(8,128)(2,1)} %param.13), kind=kOutput, calls=%fused_computation.11 | convolution fusion | flops 7519338496 | bytes 37502976 | tf_op jit(solution)/shard_map/dot_general | solution.py:40
  75.0 15.5 %convolution_convert_fusion.2 = bf16[256,3584]{1,0:T(8,128)(2,1)} fusion(bf16[256,4096]{1,0:T(8,128)(2,1)S(1)} %get-tuple-element.4, bf16[4096,3584]{1,0:T(8,128)(2,1)} %param.15), kind=kOutput, calls=%fused_computation.5 | convolution fusion | flops 7517110272 | bytes 33292288 | tf_op jit(solution)/shard_map/dot_general | solution.py:44
  90.5 56.1 %all-reduce.3.cloned.1.call-done = bf16[256,3584]{1,0:T(8,128)(2,1)} async-done(((bf16[256,3584]{1,0:T(8,128)(2,1)}), bf16[256,3584]{1,0:T(8,128)(2,1)}) %all-reduce.3.cloned.1.call-update) | async-done | bytes 1835024 | tf_op jit(solution)/shard_map/psum | solution.py:10
  146.9 79.7 %all-reduce.5.cloned.1.call-done = bf16[256,3584]{1,0:T(8,128)(2,1)} async-done(((bf16[256,3584]{1,0:T(8,128)(2,1)}), bf16[256,3584]{1,0:T(8,128)(2,1)}) %all-reduce.5.cloned.1.call-update) | async-done | bytes 1835024 | tf_op jit(solution)/shard_map/psum | solution.py:11
  226.6 4.0 convert_add_fusion
  230.6 5.6 fusion.30
  238.5 4.3 fusion.2
  244.5 64.1 %reduce-scatter.7.cloned.1.call-done = bf16[448,256]{1,0:T(8,128)(2,1)} async-done(((bf16[3584,256]{1,0:T(8,128)(2,1)}), bf16[448,256]{1,0:T(8,128)(2,1)}) %reduce-scatter.7.cloned.1.call-update) | async-done | bytes 229392
  309.8 19.4 %psum.37 = f32[256]{0:T(256)S(1)} all-reduce(f32[256]{0:T(256)S(1)} %fusion.20), channel_id=1, replica_groups=mesh['batch'=4,'tensor'=2,'latent'=4] {'tensor','latent'}, use_global_device_ids=true, to_apply=%region_5.0 | all-reduce | flops 256 | bytes 2048 | tf_op jit(solution)/shard_map/psum | solution.py:61
  330.7 17.2 %psum.38 = f32[256]{0:T(256)S(1)} all-reduce(f32[256]{0:T(256)S(1)} %fusion.16), channel_id=1, replica_groups=mesh['batch'=4,'tensor'=2,'latent'=4] {'tensor','latent'}, use_global_device_ids=true, to_apply=%region_7.0 | all-reduce | flops 256 | bytes 2048 | tf_op jit(solution)/shard_map/psum | solution.py:68
  350.4 45.8 %all-gather.8.cloned.1.call-done = bf16[256,3584]{0,1:T(8,128)(2,1)} async-done(((bf16[256,448]{0,1:T(8,128)(2,1)}), bf16[256,3584]{0,1:T(8,128)(2,1)}) %all-gather.8.cloned.1.call-update) | async-done | bytes 1835024 | tf_op jit(solution)/shard_map/all_gather | solution.py:71
  396.3 5.6 fusion.45
  401.9 5.5 fusion.21
  411.2 65.5 %reduce-scatter.9.cloned.1.call-done = bf16[448,256]{1,0:T(8,128)(2,1)} async-done(((bf16[3584,256]{1,0:T(8,128)(2,1)}), bf16[448,256]{1,0:T(8,128)(2,1)}) %reduce-scatter.9.cloned.1.call-update) | async-done | bytes 229392
  479.2 19.2 %psum.39 = f32[256]{0:T(256)S(1)} all-reduce(f32[256]{0:T(256)S(1)} %multiply_reduce_fusion.1), channel_id=1, replica_groups=mesh['batch'=4,'tensor'=2,'latent'=4] {'tensor','latent'}, use_global_device_ids=true, to_apply=%region_10.0 | all-reduce | flops 256 | bytes 2048 | tf_op jit(solution)/shard_map/psum | solution.py:88
  501.6 43.9 %all-gather.10.cloned.1.call-done = bf16[256,3584]{0,1:T(8,128)(2,1)} async-done(((bf16[256,448]{0,1:T(8,128)(2,1)}), bf16[256,3584]{0,1:T(8,128)(2,1)}) %all-gather.10.cloned.1.call-update) | async-done | bytes 1835024 | tf_op jit(solution)/shard_map/all_gather | solution.py:90
  545.5 18.3 %fusion = bf16[256,4096]{1,0:T(8,128)(2,1)} fusion(bf16[256,3584]{0,1:T(8,128)(2,1)} %all-gather.10.cloned.1.call-done, bf16[4096,3584]{1,0:T(8,128)(2,1)} %param.15, f32[256,4096]{1,0:T(8,128)} %get-tuple-element.5), kind=kOutput, calls=%fused_computation.6 | convolution fusion | flops 7519338496 | bytes 37486592 | tf_op jit(solution)/shard_map/dot_general | solution.py:91
  563.8 46.2 %all_to_all.38 = bf16[256,4,896]{0,2,1:T(8,128)(2,1)} all-to-all(bf16[256,4,896]{0,2,1:T(8,128)(2,1)S(1)} %bitcast.35), channel_id=1, replica_groups=mesh['batch'=4,'tensor'=2,'latent'=4] {'batch'}, dimensions={1} | all-to-all | bytes 3670016 | tf_op jit(solution)/shard_map/all_to_all | solution.py:96
  610.0 3.8 all-to-all-start.1
  617.5 24.1 %all-to-all-done.1 = bf16[256,4,896]{0,2,1:T(8,128)(2,1)S(1)} async-done(((bf16[256,4,896]{0,2,1:T(8,128)(2,1)}), bf16[256,4,896]{0,2,1:T(8,128)(2,1)S(1)}, u32[]{:S(2)}, u32[]{:S(2)}) %all-to-all-start.1) | async-done | bytes 1835040 | tf_op jit(solution)/shard_map/all_to_all | solution.py:97
  644.0 15.2 %convolution_convert_fusion = bf16[4096,896]{1,0:T(8,128)(2,1)} fusion(bf16[1024,4096]{1,0:T(8,128)(2,1)} %all-gather.14.cloned.1.call-done, bf16[1024,896]{1,0:T(8,128)(2,1)} %bitcast.38), kind=kOutput, calls=%fused_computation | convolution fusion | flops 7519862784 | bytes 17563648 | tf_op jit(solution)/shard_map/dot_general | solution.py:106
  659.1 33.3 %all-gather.12.cloned.1.call-done = bf16[1024,4096]{1,0:T(8,128)(2,1)} async-done(((bf16[256,4096]{1,0:T(8,128)(2,1)}), bf16[1024,4096]{1,0:T(8,128)(2,1)}) %all-gather.12.cloned.1.call-update) | async-done | bytes 8388624 | tf_op jit(solution)/shard_map/all_gather | solution.py:101
  692.4 12.1 %convolution_convert_fusion.1 = bf16[896,4096]{1,0:T(8,128)(2,1)} fusion(bf16[1024,896]{1,0:T(8,128)(2,1)S(1)} %bitcast.37, bf16[1024,4096]{1,0:T(8,128)(2,1)} %all-gather.12.cloned.1.call-done), kind=kOutput, calls=%fused_computation.1 | convolution fusion | flops 7519862784 | bytes 17563648 | tf_op jit(solution)/shard_map/dot_general | solution.py:103
  (74 shorter events, 28.1 us)
Async XLA Ops:
  7.2 52.6 %all-gather.6.cloned.1.call-start = ((), (), s32[]{:S(2)}) async-start(), calls=%async_computation.4 | async-start | bytes 2064384 | tf_op jit(solution)/shard_map/all_gather | solution.py:39
  9.8 136.8 %all-reduce.3.cloned.1.call-start = ((), (), s32[]{:S(2)}) async-start(), calls=%async_computation.5 | async-start | bytes 3670016 | tf_op jit(solution)/shard_map/psum | solution.py:10
  75.0 15.5 %copy-start = (bf16[256,4096]{1,0:T(8,128)(2,1)}, bf16[256,4096]{1,0:T(8,128)(2,1)S(1)}, u32[]{:S(2)}) copy-start(bf16[256,4096]{1,0:T(8,128)(2,1)S(1)} %get-tuple-element.4) | copy-start | bytes 6291460
  90.4 56.4 %copy-start.5 = (bf16[3584]{0:T(1024)(128)(2,1)S(1)}, bf16[3584]{0:T(1024)(128)(2,1)}, u32[]{:S(2)}) copy-start(bf16[3584]{0:T(1024)(128)(2,1)} %param.16) | copy-start | bytes 21508
  90.4 56.4 %copy-start.6 = (bf16[3584]{0:T(1024)(128)(2,1)S(1)}, bf16[3584]{0:T(1024)(128)(2,1)}, u32[]{:S(2)}) copy-start(bf16[3584]{0:T(1024)(128)(2,1)} %param.17) | copy-start | bytes 21508
  90.4 136.2 %all-reduce.5.cloned.1.call-start = ((), (), s32[]{:S(2)}) async-start(), calls=%async_computation.6 | async-start | bytes 3670016 | tf_op jit(solution)/shard_map/psum | solution.py:11
  146.6 162.0 %reduce-scatter.7.cloned.1.call-start = ((), (), s32[]{:S(2)}) async-start(), calls=%async_computation.11 | async-start | bytes 2064384
  226.6 9.6 %slice-start = ((s8[6422528]{0:T(1024)(128)(4,1)}), s8[4194304]{0:T(1024)(128)(4,1)S(1)}, s32[]{:S(2)}) async-start(s8[6422528]{0:T(1024)(128)(4,1)} %bitcast.29), calls=%async_computation.13 | async-start | bytes 8388608
  230.6 5.7 slice-start.1
  230.6 5.7 copy-start.3
  230.6 7.9 %slice-start.4 = ((s8[6422528]{0:T(1024)(128)(4,1)}), s8[4194304]{0:T(1024)(128)(4,1)S(1)}, s32[]{:S(2)}) async-start(s8[6422528]{0:T(1024)(128)(4,1)} %bitcast.41), calls=%async_computation.17 | async-start | bytes 8388608
  236.3 2.2 slice-start.5
  238.5 4.4 copy-start.4
  242.8 153.5 %all-gather.8.cloned.1.call-start = ((), (), s32[]{:S(2)}) async-start(), calls=%async_computation.7 | async-start | bytes 2064384 | tf_op jit(solution)/shard_map/all_gather | solution.py:71
  350.2 126.5 %reduce-scatter.9.cloned.1.call-start = ((), (), s32[]{:S(2)}) async-start(), calls=%async_computation.12 | async-start | bytes 2064384
  396.3 11.1 %slice-start.2 = ((s8[6422528]{0:T(1024)(128)(4,1)}), s8[2228224]{0:T(1024)(128)(4,1)S(1)}, s32[]{:S(2)}) async-start(s8[6422528]{0:T(1024)(128)(4,1)} %bitcast.31), calls=%async_computation.15 | async-start | bytes 4456448
  401.9 5.5 slice-start.3
  411.1 134.4 %all-gather.10.cloned.1.call-start = ((), (), s32[]{:S(2)}) async-start(), calls=%async_computation.8 | async-start | bytes 2064384 | tf_op jit(solution)/shard_map/all_gather | solution.py:90
  500.8 143.2 %all-gather.14.cloned.1.call-start = ((), (), s32[]{:S(2)}) async-start(), calls=%async_computation.10 | async-start | bytes 10485760 | tf_op jit(solution)/shard_map/all_gather | solution.py:100
  501.6 190.9 %all-gather.12.cloned.1.call-start = ((), (), s32[]{:S(2)}) async-start(), calls=%async_computation.9 | async-start | bytes 10485760 | tf_op jit(solution)/shard_map/all_gather | solution.py:101
  545.5 18.4 %copy-start.1 = (bf16[256,3584]{0,1:T(8,128)(2,1)S(1)}, bf16[256,3584]{0,1:T(8,128)(2,1)}, u32[]{:S(2)}) copy-start(bf16[256,3584]{0,1:T(8,128)(2,1)} %all-gather.6.cloned.1.call-done) | copy-start | bytes 5505028
  610.0 31.6 %all-to-all-start.1 = ((bf16[256,4,896]{0,2,1:T(8,128)(2,1)}), bf16[256,4,896]{0,2,1:T(8,128)(2,1)S(1)}, u32[]{:S(2)}, u32[]{:S(2)}) async-start(bf16[256,4,896]{0,2,1:T(8,128)(2,1)} %bitcast.36), calls=%async_computation.1 | async-start | bytes 3670016 | tf_op jit(solution)/shard_map/all_to_all | solution.py:97
  644.0 48.5 %copy-start.2 = (bf16[4,256,896]{2,1,0:T(8,128)(2,1)S(1)}, bf16[4,256,896]{2,1,0:T(8,128)(2,1)}, u32[]{:S(2)}) copy-start(bf16[4,256,896]{2,1,0:T(8,128)(2,1)} %copy.34) | copy-start | bytes 5505028
Sparse Core Ops, SparseCore 0:
  10.6 49.1 all-gather.5
  90.6 55.9 all-reduce.2
  149.0 77.6 all-reduce.4
  242.9 65.6 reduce-scatter.6
  350.3 45.9 all-gather.7
  411.2 65.4 reduce-scatter.8
  500.9 44.5 all-gather.9
  547.0 81.8 all-gather.13
  631.1 61.3 all-gather.11
